TPU v7x, 32 devices: a whole 2x2x4 slice. The times are simulated.
32 devices in a mesh: seq: 8 (over y, x, core), grp: 4 (over z).
Axes of the slice: x: 2, y: 2, z: 4, core: 2. Of those that a mesh axis runs over, the one named last changes fastest.
Arguments:
- queries: bfloat16 [4096, 2048], P(('seq', 'grp')), may hold values from -8 to 8
- keys: bfloat16 [4096, 128], P(('seq', 'grp')), may hold values from -8 to 8
- values: bfloat16 [4096, 128], P(('seq', 'grp')), may hold values from -6 to 6
- cotangent: bfloat16 [4096, 2048], P(('seq', 'grp')), may hold values from -6 to 6
- doc_lengths: int32 [8], replicated, may hold values from 1 to 1024, 4096 in all
Outputs:
- attn_out: bfloat16 [4096, 2048], P(('seq', 'grp'))
- grad_queries: bfloat16 [4096, 2048], P(('seq', 'grp'))
- grad_keys: bfloat16 [4096, 128], P(('seq', 'grp'))
- grad_values: bfloat16 [4096, 128], P(('seq', 'grp'))
Inputs may be any that keep to these rules, and one draw needn't show every extreme that they name: `doc_lengths`: the lengths sum to 4096, and one of them is exactly 1024.
All inputs are finite; a program needn't handle non-finite values.
Results may differ from a plain program's by a relative error of at most 0.023.
Values may be sent and summed in bfloat16 or wider, within the bound.
A program may use at most 64 MiB of HBM per device.

v0:
```python
import functools

import jax
import jax.numpy as jnp
from jax import lax
from jax.experimental import pallas as pl
from jax.experimental.pallas import tpu as pltpu
from jax.sharding import PartitionSpec as P

REACH = 8
HALF = REACH // 2
GROUP_HEADS = 4
MASKED = -1e30
LOG2E = 1.4426950408889634
PLACES = (0, 1, 3, 4, 2, 5, 6, 7, 8)


def kernel(
    count,
    members,
    lengths_hbm,
    queries_hbm,
    keys_hbm,
    values_hbm,
    cotangent_hbm,
    out_ref,
    grad_queries_ref,
    grad_keys_ref,
    grad_values_ref,
    window,
    queries_t,
    cotangent_t,
    keys_t,
    values_t,
    probs,
    grad_probs,
    peaks,
    sums,
    dots,
    row_dots,
    weights_low,
    grad_scores,
    grad_window,
    grad_send,
    grad_far,
    grad_near,
    send_sems,
    recv_sems,
    grad_send_sems,
    grad_recv_sems,
    lengths_ref,
    stacked,
    keys_ref,
    values_ref,
    load_sems,
):
    rows, head_size = keys_ref.shape
    head_count = stacked.shape[0] // rows
    heads = min(head_count, GROUP_HEADS)
    width = heads * rows
    groups = head_count // heads
    scaling = head_size ** (-0.5)
    me = lax.axis_index("seq") * members + lax.axis_index("grp")

    def place(index):
        return (lax.div(index, members), lax.rem(index, members))

    def key_copy(distance, half):
        source = (keys_ref, values_ref)[half]
        target = me + distance
        if distance > HALF:
            source = window.at[distance - HALF, half]
            target = me + HALF
        return pltpu.make_async_remote_copy(
            src_ref=source,
            dst_ref=window.at[distance, half],
            send_sem=send_sems.at[distance, half],
            recv_sem=recv_sems.at[distance, half],
            device_id=place(target),
            device_id_type=pl.DeviceIdType.MESH,
        )

    def grad_copy(distance):
        if distance > HALF:
            target, slot = me - HALF, grad_far.at[distance - HALF]
        else:
            target, slot = me - distance, grad_near.at[distance]
        return pltpu.make_async_remote_copy(
            src_ref=grad_send.at[distance],
            dst_ref=slot,
            send_sem=grad_send_sems.at[distance],
            recv_sem=grad_recv_sems.at[distance],
            device_id=place(target),
            device_id_type=pl.DeviceIdType.MESH,
        )

    pairs = [
        (keys_hbm, keys_ref),
        (values_hbm, values_ref),
        (lengths_hbm, lengths_ref),
    ]
    for half, source in enumerate((queries_hbm, cotangent_hbm)):
        for head in range(head_count):
            pairs.append(
                (
                    source.at[:, head * head_size : (head + 1) * head_size],
                    stacked.at[
                        head * rows : (head + 1) * rows,
                        half * head_size : (half + 1) * head_size,
                    ],
                )
            )
    loads = [
        pltpu.make_async_copy(source, target, load_sems.at[index])
        for index, (source, target) in enumerate(pairs)
    ]
    for load in loads:
        load.start()

    barrier = pltpu.get_barrier_semaphore()
    for distance in range(1, HALF + 1):
        for there in (me + distance, me - distance):

            @pl.when((there >= 0) & (there < count))
            def _():
                pl.semaphore_signal(
                    barrier, inc=1, device_id=place(there), device_id_type=pl.DeviceIdType.MESH
                )

    for distance in range(1, REACH + 1):

        @pl.when(me < distance)
        def _():
            window[distance] = jnp.zeros_like(window.at[distance])

    for distance in range(1, HALF + 1):

        @pl.when(me + distance >= count)
        def _():
            grad_near[distance] = jnp.zeros_like(grad_near.at[distance])

        @pl.when((me + HALF >= count) | (me < distance))
        def _():
            grad_far[distance] = jnp.zeros_like(grad_far.at[distance])

    for load in loads[:3]:
        load.wait()
    query_pos = me * rows + lax.broadcasted_iota(jnp.int32, (1, rows), 1)

    def one_doc(doc, state):
        end, start = state
        end = end + lengths_ref[doc]
        return end, jnp.where(query_pos >= end, end, start)

    _, doc_start = lax.fori_loop(
        0, lengths_ref.shape[0], one_doc, (jnp.int32(0), jnp.zeros((1, rows), jnp.int32))
    )

    for load in loads[3:]:
        load.wait()
    for head in range(head_count):
        columns = slice(head * rows, (head + 1) * rows)
        queries_t[:, columns] = stacked[columns, 0:head_size].T
        cotangent_t[:, columns] = stacked[columns, head_size:].T

    def block_rows(distance):
        return slice(PLACES[distance] * rows, (PLACES[distance] + 1) * rows)

    def block_of(distance):
        if distance == 0:
            return keys_ref[...], values_ref[...]
        return window[distance, 0], window[distance, 1]

    def score_block(distance):
        keys, values = block_of(distance)
        span = block_rows(distance)
        keys_t[:, span] = keys.T
        values_t[:, span] = values.T
        key_pos = (me - distance) * rows + lax.broadcasted_iota(jnp.int32, (rows, rows), 0)
        allowed = key_pos >= doc_start
        if distance == 0:
            allowed = allowed & (key_pos <= query_pos)
        bias = jnp.where(allowed, 0.0, MASKED).astype(jnp.float32)
        bias = jnp.concatenate([bias] * heads, axis=1)

        def folded(part, op):
            return op(part.reshape(rows // 8, 8, width), axis=0)

        for group in range(groups):
            columns = slice(group * width, (group + 1) * width)
            scores = jnp.dot(keys, queries_t[:, columns], preferred_element_type=jnp.float32)
            scores = scores * (scaling * LOG2E) + bias
            peak = folded(scores, jnp.max)
            prob = jnp.exp2(scores.reshape(rows // 8, 8, width) - peak[None]).reshape(rows, width)
            grad_prob = jnp.dot(values, cotangent_t[:, columns], preferred_element_type=jnp.float32)
            probs[span, columns] = prob
            grad_probs[span, columns] = grad_prob
            peaks[distance, :, columns] = peak
            sums[distance, :, columns] = folded(prob, jnp.sum)
            dots[distance, :, columns] = folded(prob * grad_prob, jnp.sum)

    score_block(0)
    pl.semaphore_wait(barrier, jnp.minimum(me, HALF) + jnp.minimum(count - 1 - me, HALF))

    for distance in (4, 3, 2, 1):

        @pl.when(me + distance < count)
        def _():
            for half in range(2):
                key_copy(distance, half).start()

    for distance in (4, 1, 2, 3):

        @pl.when(me >= distance)
        def _():
            for half in range(2):
                key_copy(distance, half).wait_recv()

        @pl.when((me >= distance) & (me + HALF < count))
        def _():
            for half in range(2):
                key_copy(distance + HALF, half).start()

        score_block(distance)
    for distance in (8, 5, 6, 7):

        @pl.when(me >= distance)
        def _():
            for half in range(2):
                key_copy(distance, half).wait_recv()

        score_block(distance)

    for group in range(groups):
        columns = slice(group * width, (group + 1) * width)
        top = peaks[0, :, columns]
        for distance in range(1, REACH + 1):
            top = jnp.maximum(top, peaks[distance, :, columns])
        top = jnp.max(top, axis=0, keepdims=True)
        total = jnp.zeros((8, width), jnp.float32)
        dot = total
        for distance in range(REACH + 1):
            factor = jnp.exp2(peaks[distance, :, columns] - top)
            peaks[distance, :, columns] = factor
            total = total + factor * sums[distance, :, columns]
            dot = dot + factor * dots[distance, :, columns]
        inverse = 1.0 / jnp.sum(total, axis=0, keepdims=True)
        row_dots[:, columns] = jnp.broadcast_to(
            jnp.sum(dot, axis=0, keepdims=True) * inverse, (8, width)
        )
        for distance in range(REACH + 1):
            peaks[distance, :, columns] = peaks[distance, :, columns] * inverse

    def grad_blocks(distances):
        size = len(distances) * rows
        first = PLACES[distances[0]]
        span = slice(first * rows, first * rows + size)
        tiles = (rows // 8, 8, width)
        for group in range(groups):
            columns = slice(group * width, (group + 1) * width)
            row_dot = row_dots[:, columns]
            for distance in distances:
                block = block_rows(distance)
                weights = probs[block, columns].reshape(tiles) * peaks[distance, :, columns][None]
                weights_low[block, columns] = weights.reshape(rows, width).astype(jnp.bfloat16)
                grads = weights * (grad_probs[block, columns].reshape(tiles) - row_dot[None])
                grad_scores[block, columns] = grads.reshape(rows, width).astype(jnp.bfloat16)
        for half, left in enumerate((grad_scores, weights_low)):
            both = jnp.dot(left[span, :], stacked[...], preferred_element_type=jnp.float32)
            grad_window[half, span, :] = both[:, half * head_size : (half + 1) * head_size]

    grad_blocks((5, 6, 7, 8))
    for distance in range(REACH, HALF, -1):
        block = block_rows(distance)

        @pl.when(me >= distance)
        def _():
            for half in range(2):
                grad_send[distance, half] = grad_window[half, block, :].astype(jnp.bfloat16)
            grad_copy(distance).start()

    def send_near(distance):
        block = block_rows(distance)

        @pl.when((me >= distance) & (me + HALF < count))
        def _():
            grad_copy(distance + HALF).wait_recv()

        @pl.when(me >= distance)
        def _():
            for half in range(2):
                grad_send[distance, half] = (
                    grad_window[half, block, :] + grad_far[distance, half].astype(jnp.float32)
                ).astype(jnp.bfloat16)
            grad_copy(distance).start()

    for distances in ((2, 3), (1, 4)):
        grad_blocks(distances)
        for distance in reversed(distances):
            send_near(distance)

    grad_blocks((0,))
    for group in range(groups):
        columns = slice(group * width, (group + 1) * width)
        out_part = jnp.dot(
            values_t[...], weights_low[:, columns], preferred_element_type=jnp.float32
        ).astype(jnp.bfloat16)
        grad_part = jnp.dot(
            keys_t[...], grad_scores[:, columns], preferred_element_type=jnp.float32
        )
        grad_part = (grad_part * scaling).astype(jnp.bfloat16)
        for head in range(heads):
            local = slice(head * rows, (head + 1) * rows)
            first = (group * heads + head) * head_size
            out_ref[:, first : first + head_size] = out_part[:, local].T
            grad_queries_ref[:, first : first + head_size] = grad_part[:, local].T

    for distance in range(1, HALF + 1):

        @pl.when(me + distance < count)
        def _():
            grad_copy(distance).wait_recv()

    owned = []
    for half in range(2):
        part = grad_window[half, 0:rows, :]
        for distance in range(1, HALF + 1):
            part = part + grad_near[distance, half].astype(jnp.float32)
        owned.append(part)
    grad_keys_ref[...] = (owned[0] * scaling).astype(jnp.bfloat16)
    grad_values_ref[...] = owned[1].astype(jnp.bfloat16)

    for distance in range(1, REACH + 1):
        reachable = me + distance < count
        if distance > HALF:
            reachable = (me >= distance - HALF) & (me + HALF < count)

        @pl.when(reachable)
        def _():
            for half in range(2):
                key_copy(distance, half).wait_send()

        @pl.when(me >= distance)
        def _():
            grad_copy(distance).wait_send()


def settle(*refs):
    half = len(refs) // 2
    for source, target in zip(refs[:half], refs[half:]):
        target[...] = source[...]


def per_device(queries, keys, values, cotangent, doc_lengths):
    rows, head_size = keys.shape
    head_count = queries.shape[1] // head_size
    members = lax.axis_size("grp")
    count = lax.axis_size("seq") * members
    tall = (REACH + 1) * rows
    wide = head_count * rows
    vmem = pl.BlockSpec(memory_space=pltpu.VMEM)
    far = pl.BlockSpec(memory_space=pltpu.HBM)
    low, full = jnp.bfloat16, jnp.float32
    results = pl.pallas_call(
        functools.partial(kernel, count, members),
        out_shape=(
            jax.ShapeDtypeStruct(queries.shape, low),
            jax.ShapeDtypeStruct(queries.shape, low),
            jax.ShapeDtypeStruct(keys.shape, low),
            jax.ShapeDtypeStruct(keys.shape, low),
        ),
        in_specs=[far] * 5,
        out_specs=(vmem,) * 4,
        scratch_shapes=[
            pltpu.VMEM((REACH + 1, 2, rows, head_size), low),
            pltpu.VMEM((head_size, wide), low),
            pltpu.VMEM((head_size, wide), low),
            pltpu.VMEM((head_size, tall), low),
            pltpu.VMEM((head_size, tall), low),
            pltpu.VMEM((tall, wide), full),
            pltpu.VMEM((tall, wide), full),
            pltpu.VMEM((REACH + 1, 8, wide), full),
            pltpu.VMEM((REACH + 1, 8, wide), full),
            pltpu.VMEM((REACH + 1, 8, wide), full),
            pltpu.VMEM((8, wide), full),
            pltpu.VMEM((tall, wide), low),
            pltpu.VMEM((tall, wide), low),
            pltpu.VMEM((2, tall, head_size), full),
            pltpu.VMEM((REACH + 1, 2, rows, head_size), low),
            pltpu.VMEM((HALF + 1, 2, rows, head_size), low),
            pltpu.VMEM((HALF + 1, 2, rows, head_size), low),
            pltpu.SemaphoreType.DMA((REACH + 1, 2)),
            pltpu.SemaphoreType.DMA((REACH + 1, 2)),
            pltpu.SemaphoreType.DMA((REACH + 1,)),
            pltpu.SemaphoreType.DMA((REACH + 1,)),
            pltpu.SMEM(doc_lengths.shape, jnp.int32),
            pltpu.VMEM((wide, 2 * head_size), low),
            pltpu.VMEM(keys.shape, low),
            pltpu.VMEM(keys.shape, low),
            pltpu.SemaphoreType.DMA((3 + 2 * head_count,)),
        ],
        compiler_params=pltpu.CompilerParams(
            collective_id=0, has_side_effects=True, vmem_limit_bytes=60 * 1024 * 1024
        ),
        name="attention",
    )(doc_lengths, queries, keys, values, cotangent)
    return pl.pallas_call(
        settle,
        out_shape=tuple(jax.ShapeDtypeStruct(result.shape, low) for result in results),
        in_specs=[vmem] * 4,
        out_specs=(vmem,) * 4,
        compiler_params=pltpu.CompilerParams(vmem_limit_bytes=60 * 1024 * 1024),
        name="settle",
    )(*results)


def solution(mesh):
    rows = P(("seq", "grp"), None)
    return jax.shard_map(
        per_device,
        mesh=mesh,
        in_specs=(rows, rows, rows, rows, P()),
        out_specs=(rows, rows, rows, rows),
        check_vma=False,
    )
```

profile of v0, /device:TPU:1, one launch (start us, length us, event | category | flops | bytes accessed | tf_op | source)
XLA Modules:
  0.0 31.1 jit_solution(13259107624390462948)
XLA Ops:
  0.6 28.3 %attention.1 = (bf16[128,2048]{1,0:T(8,128)(2,1)}, bf16[128,2048]{1,0:T(8,128)(2,1)}, bf16[128,128]{1,0:T(8,128)(2,1)}, bf16[128,128]{1,0:T(8,128)(2,1)}) custom-call(s32[8]{0:T(128)} %lengths_hbm.1, bf16[128,2048]{1,0:T(8,128)(2,1)} %queries_hbm.1, bf16[128,128]{1,0:T(8,128)(2,1)} %keys_hbm.1, bf16[128,128]{1,0:T(8,128)(2,1)} %values_hbm.1, ...), custom_call_target="tpu_custom_call" | custom-call | tf_op jit(solution)/shard_map/attention/pallas_call | solution.py:364
  28.9 2.2 %settle.1 = (bf16[128,2048]{1,0:T(8,128)(2,1)}, bf16[128,2048]{1,0:T(8,128)(2,1)}, bf16[128,128]{1,0:T(8,128)(2,1)}, bf16[128,128]{1,0:T(8,128)(2,1)}) custom-call(bf16[128,2048]{1,0:T(8,128)(2,1)} %get-tuple-element.8.refs_0_, bf16[128,2048]{1,0:T(8,128)(2,1)} %get-tuple-element.9.refs_1_, bf16[128,128]{1,0:T(8,128)(2,1)} %get-tuple-element.10.refs_2_, ...), custom_call_target="tpu_custom_call" | custom-call | tf_op jit(solution)/shard_map/settle/pallas_call | solution.py:407
where the time goes:
time: 31.5 us; the launch traced here: 31.1 us
  Pallas kernels  30.5 us (97%)
  between operations  0.64 us (2%)
    pallas_call x1, Pallas kernels, per_device(): pl.pallas_call(functools.partial(kernel, count, members), out_shape=(jax....  28.3 us
    pallas_call x1, Pallas kernels, per_device(): pl.pallas_call(settle, out_shape=tuple((jax.ShapeDtypeStruct(result.shape...  2.21 us

commit v1 on v0

--- a/solution.py
+++ b/solution.py
@@ -65,20 +65,56 @@
     def place(index):
         return (lax.div(index, members), lax.rem(index, members))
 
-    def key_copy(distance, half):
-        source = (keys_ref, values_ref)[half]
-        target = me + distance
-        if distance > HALF:
-            source = window.at[distance - HALF, half]
-            target = me + HALF
+    member = lax.axis_index("grp")
+    paired = members == HALF
+
+    def key_copy(distance, half, step=None):
+        if step is not None:
+            source, slot, sender = window.at[distance, half], distance + step, 0
+        elif distance > HALF:
+            source, slot, sender = window.at[distance - HALF, half], distance, distance
+            step = HALF
+        else:
+            source, slot, sender = (keys_ref, values_ref)[half], distance, distance
+            step = distance
         return pltpu.make_async_remote_copy(
             src_ref=source,
-            dst_ref=window.at[distance, half],
-            send_sem=send_sems.at[distance, half],
-            recv_sem=recv_sems.at[distance, half],
-            device_id=place(target),
+            dst_ref=window.at[slot, half],
+            send_sem=send_sems.at[sender, half],
+            recv_sem=recv_sems.at[slot, half],
+            device_id=place(me + step),
             device_id_type=pl.DeviceIdType.MESH,
         )
+
+    def direct(distance, sender):
+        within = (sender >= 0) & (sender + distance < count)
+        if paired and distance == 1:
+            within = within & (lax.rem(sender + members, members) <= members - 2)
+        if paired and distance == HALF - 1:
+            within = within & (lax.rem(sender + members, members) >= 1)
+        return within
+
+    turns = ()
+    if paired:
+        middle = HALF // 2
+        turns = (
+            ((member == middle - 1) & (me >= middle), middle, -1),
+            (member == middle, middle, 1),
+        )
+
+    def pass_on(distance):
+        for fits, slot, step in turns:
+            if slot == distance:
+
+                @pl.when(fits)
+                def _():
+                    for half in range(2):
+                        key_copy(distance, half, step).start()
+
+        @pl.when((me >= distance) & (me + HALF < count))
+        def _():
+            for half in range(2):
+                key_copy(distance + HALF, half).start()
 
     def grad_copy(distance):
         if distance > HALF:
@@ -118,10 +154,15 @@
         load.start()
 
     barrier = pltpu.get_barrier_semaphore()
-    for distance in range(1, HALF + 1):
-        for there in (me + distance, me - distance):
-
-            @pl.when((there >= 0) & (there < count))
+    greeted = jnp.int32(0)
+    for distance in range(HALF, 0, -1):
+        for fits, there in (
+            (direct(distance, me), me + distance),
+            (direct(distance, me - distance), me - distance),
+        ):
+            greeted = greeted + fits.astype(jnp.int32)
+
+            @pl.when(fits)
             def _():
                 pl.semaphore_signal(
                     barrier, inc=1, device_id=place(there), device_id_type=pl.DeviceIdType.MESH
@@ -200,35 +241,23 @@
             dots[distance, :, columns] = folded(prob * grad_prob, jnp.sum)
 
     score_block(0)
-    pl.semaphore_wait(barrier, jnp.minimum(me, HALF) + jnp.minimum(count - 1 - me, HALF))
-
-    for distance in (4, 3, 2, 1):
-
-        @pl.when(me + distance < count)
+    pl.semaphore_wait(barrier, greeted)
+    for distance in (4, 2, 1, 3):
+
+        @pl.when(direct(distance, me))
         def _():
             for half in range(2):
                 key_copy(distance, half).start()
 
-    for distance in (4, 1, 2, 3):
+    for distance in (4, 2, 1, 3, 8, 6, 5, 7):
 
         @pl.when(me >= distance)
         def _():
             for half in range(2):
                 key_copy(distance, half).wait_recv()
 
-        @pl.when((me >= distance) & (me + HALF < count))
-        def _():
-            for half in range(2):
-                key_copy(distance + HALF, half).start()
-
-        score_block(distance)
-    for distance in (8, 5, 6, 7):
-
-        @pl.when(me >= distance)
-        def _():
-            for half in range(2):
-                key_copy(distance, half).wait_recv()
-
+        if distance <= HALF:
+            pass_on(distance)
         score_block(distance)
 
     for group in range(groups):
@@ -331,11 +360,11 @@
     grad_values_ref[...] = owned[1].astype(jnp.bfloat16)
 
     for distance in range(1, REACH + 1):
-        reachable = me + distance < count
+        sent = direct(distance, me)
         if distance > HALF:
-            reachable = (me >= distance - HALF) & (me + HALF < count)
-
-        @pl.when(reachable)
+            sent = (me >= distance - HALF) & (me + HALF < count)
+
+        @pl.when(sent)
         def _():
             for half in range(2):
                 key_copy(distance, half).wait_send()
@@ -344,11 +373,23 @@
         def _():
             grad_copy(distance).wait_send()
 
+    for fits, slot, step in turns:
+
+        @pl.when(fits)
+        def _():
+            for half in range(2):
+                key_copy(slot, half, step).wait_send()
+
 
 def settle(*refs):
-    half = len(refs) // 2
-    for source, target in zip(refs[:half], refs[half:]):
-        target[...] = source[...]
+    copies = [
+        pltpu.make_async_copy(refs[index], refs[4 + index], refs[8].at[index])
+        for index in range(4)
+    ]
+    for copy in copies:
+        copy.start()
+    for copy in copies:
+        copy.wait()
 
 
 def per_device(queries, keys, values, cotangent, doc_lengths):
@@ -361,13 +402,11 @@
     vmem = pl.BlockSpec(memory_space=pltpu.VMEM)
     far = pl.BlockSpec(memory_space=pltpu.HBM)
     low, full = jnp.bfloat16, jnp.float32
+    operands = (doc_lengths, queries, keys, values, cotangent)
     results = pl.pallas_call(
         functools.partial(kernel, count, members),
-        out_shape=(
-            jax.ShapeDtypeStruct(queries.shape, low),
-            jax.ShapeDtypeStruct(queries.shape, low),
-            jax.ShapeDtypeStruct(keys.shape, low),
-            jax.ShapeDtypeStruct(keys.shape, low),
+        out_shape=tuple(
+            pltpu.VMEM(part.shape, low) for part in (queries, queries, keys, keys)
         ),
         in_specs=[far] * 5,
         out_specs=(vmem,) * 4,
@@ -400,16 +439,17 @@
             pltpu.SemaphoreType.DMA((3 + 2 * head_count,)),
         ],
         compiler_params=pltpu.CompilerParams(
-            collective_id=0, has_side_effects=True, vmem_limit_bytes=60 * 1024 * 1024
+            collective_id=0, has_side_effects=True, vmem_limit_bytes=50000 * 1024
         ),
         name="attention",
-    )(doc_lengths, queries, keys, values, cotangent)
+    )(*(pltpu.with_memory_space_constraint(part, pltpu.HBM) for part in operands))
     return pl.pallas_call(
         settle,
         out_shape=tuple(jax.ShapeDtypeStruct(result.shape, low) for result in results),
         in_specs=[vmem] * 4,
-        out_specs=(vmem,) * 4,
-        compiler_params=pltpu.CompilerParams(vmem_limit_bytes=60 * 1024 * 1024),
+        out_specs=(far,) * 4,
+        scratch_shapes=[pltpu.SemaphoreType.DMA((4,))],
+        compiler_params=pltpu.CompilerParams(vmem_limit_bytes=4096 * 1024),
         name="settle",
     )(*results)
 

time: 31.5 us -> 28.5 us (0.905)
  Pallas kernels: 30.5 us -> 27.6 us
    pallas_call x1, Pallas kernels: 28.3 us -> 26.6 us  [per_device(): pl.pallas_call(functools.partial(kernel, count, members), out_shape=tuple...]
    pallas_call x1, Pallas kernels: 2.21 us -> 1.01 us  [per_device(): pl.pallas_call(settle, out_shape=tuple((jax.ShapeDtypeStruct(result.shape...]
where the time goes in v1:
time: 28.5 us; the launch traced here: 28.2 us
  Pallas kernels  27.6 us (97%)
  between operations  0.64 us (2%)
    pallas_call x1, Pallas kernels, per_device(): pl.pallas_call(functools.partial(kernel, count, members), out_shape=tuple...  26.6 us
    pallas_call x1, Pallas kernels, per_device(): pl.pallas_call(settle, out_shape=tuple((jax.ShapeDtypeStruct(result.shape...  1.01 us

profile of v1, /device:TPU:1, one launch (start us, length us, event | category | flops | bytes accessed | tf_op | source)
XLA Modules:
  0.0 28.2 jit_solution(4808661099151765816)
XLA Ops:
  0.6 26.6 %attention.1 = (bf16[128,2048]{1,0:T(8,128)(2,1)S(1)}, bf16[128,2048]{1,0:T(8,128)(2,1)S(1)}, bf16[128,128]{1,0:T(8,128)(2,1)S(1)}, bf16[128,128]{1,0:T(8,128)(2,1)S(1)}) custom-call(s32[8]{0:T(128)} %lengths_hbm.1, bf16[128,2048]{1,0:T(8,128)(2,1)} %queries_hbm.1, bf16[128,128]{1,0:T(8,128)(2,1)} %keys_hbm.1, bf16[128,128]{1,0:T(8,128)(2,1)} %values_hbm.1, ...), custom_call_target="tpu_custom_call" | custom-call | tf_op jit(solution)/shard_map/attention/pallas_call | solution.py:406
  27.2 1.0 %settle.1 = (bf16[128,2048]{1,0:T(8,128)(2,1)}, bf16[128,2048]{1,0:T(8,128)(2,1)}, bf16[128,128]{1,0:T(8,128)(2,1)}, bf16[128,128]{1,0:T(8,128)(2,1)}) custom-call(bf16[128,2048]{1,0:T(8,128)(2,1)S(1)} %get-tuple-element.8.refs_0_, bf16[128,2048]{1,0:T(8,128)(2,1)S(1)} %get-tuple-element.9.refs_1_, bf16[128,128]{1,0:T(8,128)(2,1)S(1)} %get-tuple-element.10.refs_2_, ...), custom_call_target="tpu_custom_call" | custom-call | tf_op jit(solution)/shard_map/settle/pallas_call | solution.py:446

commit v2 on v1

--- a/solution.py
+++ b/solution.py
@@ -102,30 +102,28 @@
             (member == middle, middle, 1),
         )
 
-    def pass_on(distance):
+    def pass_on(distance, half):
         for fits, slot, step in turns:
             if slot == distance:
 
                 @pl.when(fits)
                 def _():
-                    for half in range(2):
-                        key_copy(distance, half, step).start()
+                    key_copy(distance, half, step).start()
 
         @pl.when((me >= distance) & (me + HALF < count))
         def _():
-            for half in range(2):
-                key_copy(distance + HALF, half).start()
-
-    def grad_copy(distance):
+            key_copy(distance + HALF, half).start()
+
+    def grad_copy(distance, half):
         if distance > HALF:
-            target, slot = me - HALF, grad_far.at[distance - HALF]
+            target, slot = me - HALF, grad_far.at[distance - HALF, half]
         else:
-            target, slot = me - distance, grad_near.at[distance]
+            target, slot = me - distance, grad_near.at[distance, half]
         return pltpu.make_async_remote_copy(
-            src_ref=grad_send.at[distance],
+            src_ref=grad_send.at[distance, half],
             dst_ref=slot,
-            send_sem=grad_send_sems.at[distance],
-            recv_sem=grad_recv_sems.at[distance],
+            send_sem=grad_send_sems.at[distance, half],
+            recv_sem=grad_recv_sems.at[distance, half],
             device_id=place(target),
             device_id_type=pl.DeviceIdType.MESH,
         )
@@ -150,7 +148,7 @@
         pltpu.make_async_copy(source, target, load_sems.at[index])
         for index, (source, target) in enumerate(pairs)
     ]
-    for load in loads:
+    for load in loads[:2]:
         load.start()
 
     barrier = pltpu.get_barrier_semaphore()
@@ -167,6 +165,9 @@
                 pl.semaphore_signal(
                     barrier, inc=1, device_id=place(there), device_id_type=pl.DeviceIdType.MESH
                 )
+
+    for load in loads[2:]:
+        load.start()
 
     for distance in range(1, REACH + 1):
 
@@ -249,15 +250,15 @@
             for half in range(2):
                 key_copy(distance, half).start()
 
-    for distance in (4, 2, 1, 3, 8, 6, 5, 7):
-
-        @pl.when(me >= distance)
-        def _():
-            for half in range(2):
+    for distance in (4, 2, 3, 1, 8, 6, 7, 5):
+        for half in range(2):
+
+            @pl.when(me >= distance)
+            def _():
                 key_copy(distance, half).wait_recv()
 
-        if distance <= HALF:
-            pass_on(distance)
+            if distance <= HALF:
+                pass_on(distance, half)
         score_block(distance)
 
     for group in range(groups):
@@ -280,56 +281,46 @@
         for distance in range(REACH + 1):
             peaks[distance, :, columns] = peaks[distance, :, columns] * inverse
 
-    def grad_blocks(distances):
-        size = len(distances) * rows
-        first = PLACES[distances[0]]
-        span = slice(first * rows, first * rows + size)
+    def grad_block(distance):
+        block = block_rows(distance)
         tiles = (rows // 8, 8, width)
         for group in range(groups):
             columns = slice(group * width, (group + 1) * width)
-            row_dot = row_dots[:, columns]
-            for distance in distances:
-                block = block_rows(distance)
-                weights = probs[block, columns].reshape(tiles) * peaks[distance, :, columns][None]
-                weights_low[block, columns] = weights.reshape(rows, width).astype(jnp.bfloat16)
-                grads = weights * (grad_probs[block, columns].reshape(tiles) - row_dot[None])
-                grad_scores[block, columns] = grads.reshape(rows, width).astype(jnp.bfloat16)
+            weights = probs[block, columns].reshape(tiles) * peaks[distance, :, columns][None]
+            weights_low[block, columns] = weights.reshape(rows, width).astype(jnp.bfloat16)
+            grads = weights * (
+                grad_probs[block, columns].reshape(tiles) - row_dots[:, columns][None]
+            )
+            grad_scores[block, columns] = grads.reshape(rows, width).astype(jnp.bfloat16)
         for half, left in enumerate((grad_scores, weights_low)):
-            both = jnp.dot(left[span, :], stacked[...], preferred_element_type=jnp.float32)
-            grad_window[half, span, :] = both[:, half * head_size : (half + 1) * head_size]
-
-    grad_blocks((5, 6, 7, 8))
-    for distance in range(REACH, HALF, -1):
-        block = block_rows(distance)
-
+            part = jnp.dot(left[block, :], stacked[:, half * head_size : (half + 1) * head_size], preferred_element_type=jnp.float32)
+            if distance > HALF:
+                grad_send[distance, half] = part.astype(jnp.bfloat16)
+            else:
+                grad_window[half, block, :] = part
+
+    def send_far(distance):
         @pl.when(me >= distance)
         def _():
             for half in range(2):
-                grad_send[distance, half] = grad_window[half, block, :].astype(jnp.bfloat16)
-            grad_copy(distance).start()
+                grad_copy(distance, half).start()
 
     def send_near(distance):
         block = block_rows(distance)
-
-        @pl.when((me >= distance) & (me + HALF < count))
-        def _():
-            grad_copy(distance + HALF).wait_recv()
-
-        @pl.when(me >= distance)
-        def _():
-            for half in range(2):
+        for half in range(2):
+
+            @pl.when((me >= distance) & (me + HALF < count))
+            def _():
+                grad_copy(distance + HALF, half).wait_recv()
+
+            @pl.when(me >= distance)
+            def _():
                 grad_send[distance, half] = (
                     grad_window[half, block, :] + grad_far[distance, half].astype(jnp.float32)
                 ).astype(jnp.bfloat16)
-            grad_copy(distance).start()
-
-    for distances in ((2, 3), (1, 4)):
-        grad_blocks(distances)
-        for distance in reversed(distances):
-            send_near(distance)
-
-    grad_blocks((0,))
-    for group in range(groups):
+                grad_copy(distance, half).start()
+
+    def finish(group):
         columns = slice(group * width, (group + 1) * width)
         out_part = jnp.dot(
             values_t[...], weights_low[:, columns], preferred_element_type=jnp.float32
@@ -344,11 +335,31 @@
             out_ref[:, first : first + head_size] = out_part[:, local].T
             grad_queries_ref[:, first : first + head_size] = grad_part[:, local].T
 
+    for distance in (7, 6, 5, 8):
+        grad_block(distance)
+        send_far(distance)
+    grad_block(3)
+    grad_block(2)
+    grad_block(1)
+    send_near(3)
+    grad_block(4)
+    grad_block(0)
+    send_near(2)
+    pending = list(range(groups))
+    early = groups // 2
+    for group in pending[:early]:
+        finish(group)
+    send_near(1)
+    for group in pending[early:]:
+        finish(group)
+    send_near(4)
+
     for distance in range(1, HALF + 1):
 
         @pl.when(me + distance < count)
         def _():
-            grad_copy(distance).wait_recv()
+            for half in range(2):
+                grad_copy(distance, half).wait_recv()
 
     owned = []
     for half in range(2):
@@ -371,7 +382,8 @@
 
         @pl.when(me >= distance)
         def _():
-            grad_copy(distance).wait_send()
+            for half in range(2):
+                grad_copy(distance, half).wait_send()
 
     for fits, slot, step in turns:
 
@@ -430,8 +442,8 @@
             pltpu.VMEM((HALF + 1, 2, rows, head_size), low),
             pltpu.SemaphoreType.DMA((REACH + 1, 2)),
             pltpu.SemaphoreType.DMA((REACH + 1, 2)),
-            pltpu.SemaphoreType.DMA((REACH + 1,)),
-            pltpu.SemaphoreType.DMA((REACH + 1,)),
+            pltpu.SemaphoreType.DMA((REACH + 1, 2)),
+            pltpu.SemaphoreType.DMA((REACH + 1, 2)),
             pltpu.SMEM(doc_lengths.shape, jnp.int32),
             pltpu.VMEM((wide, 2 * head_size), low),
             pltpu.VMEM(keys.shape, low),

time: 28.5 us -> 27.4 us (0.961); the launches traced: 28.2 us -> 26.9 us
  Pallas kernels: 27.6 us -> 26.2 us
    pallas_call x1, Pallas kernels: 26.6 us -> 25.2 us  [per_device(): pl.pallas_call(functools.partial(kernel, count, members), out_shape=tuple...]
where the time goes in v2:
time: 27.4 us; the launch traced here: 26.9 us
  Pallas kernels  26.2 us (96%)
  between operations  0.64 us (2%)
    pallas_call x1, Pallas kernels, per_device(): pl.pallas_call(functools.partial(kernel, count, members), out_shape=tuple...  25.2 us
    pallas_call x1, Pallas kernels, per_device(): pl.pallas_call(settle, out_shape=tuple((jax.ShapeDtypeStruct(result.shape...  1.01 us

profile of v2, /device:TPU:1, one launch (start us, length us, event | category | flops | bytes accessed | tf_op | source)
XLA Modules:
  0.0 26.9 jit_solution(14672906359553283971)
XLA Ops:
  0.6 25.2 %attention.1 = (bf16[128,2048]{1,0:T(8,128)(2,1)S(1)}, bf16[128,2048]{1,0:T(8,128)(2,1)S(1)}, bf16[128,128]{1,0:T(8,128)(2,1)S(1)}, bf16[128,128]{1,0:T(8,128)(2,1)S(1)}) custom-call(s32[8]{0:T(128)} %lengths_hbm.1, bf16[128,2048]{1,0:T(8,128)(2,1)} %queries_hbm.1, bf16[128,128]{1,0:T(8,128)(2,1)} %keys_hbm.1, bf16[128,128]{1,0:T(8,128)(2,1)} %values_hbm.1, ...), custom_call_target="tpu_custom_call" | custom-call | tf_op jit(solution)/shard_map/attention/pallas_call | solution.py:418
  25.8 1.0 %settle.1 = (bf16[128,2048]{1,0:T(8,128)(2,1)}, bf16[128,2048]{1,0:T(8,128)(2,1)}, bf16[128,128]{1,0:T(8,128)(2,1)}, bf16[128,128]{1,0:T(8,128)(2,1)}) custom-call(bf16[128,2048]{1,0:T(8,128)(2,1)S(1)} %get-tuple-element.8.refs_0_, bf16[128,2048]{1,0:T(8,128)(2,1)S(1)} %get-tuple-element.9.refs_1_, bf16[128,128]{1,0:T(8,128)(2,1)S(1)} %get-tuple-element.10.refs_2_, ...), custom_call_target="tpu_custom_call" | custom-call | tf_op jit(solution)/shard_map/settle/pallas_call | solution.py:458

commit v3 on v2

--- a/solution.py
+++ b/solution.py
@@ -281,23 +281,31 @@
         for distance in range(REACH + 1):
             peaks[distance, :, columns] = peaks[distance, :, columns] * inverse
 
-    def grad_block(distance):
-        block = block_rows(distance)
+    def grad_blocks(*distances):
+        first = min(PLACES[distance] for distance in distances)
+        span = slice(first * rows, (first + len(distances)) * rows)
         tiles = (rows // 8, 8, width)
         for group in range(groups):
             columns = slice(group * width, (group + 1) * width)
-            weights = probs[block, columns].reshape(tiles) * peaks[distance, :, columns][None]
-            weights_low[block, columns] = weights.reshape(rows, width).astype(jnp.bfloat16)
-            grads = weights * (
-                grad_probs[block, columns].reshape(tiles) - row_dots[:, columns][None]
-            )
-            grad_scores[block, columns] = grads.reshape(rows, width).astype(jnp.bfloat16)
+            for distance in distances:
+                block = block_rows(distance)
+                factor = peaks[distance, :, columns][None]
+                weights = probs[block, columns].reshape(tiles) * factor
+                weights_low[block, columns] = weights.reshape(rows, width).astype(jnp.bfloat16)
+                grads = weights * (
+                    grad_probs[block, columns].reshape(tiles) - row_dots[:, columns][None]
+                )
+                grad_scores[block, columns] = grads.reshape(rows, width).astype(jnp.bfloat16)
         for half, left in enumerate((grad_scores, weights_low)):
-            part = jnp.dot(left[block, :], stacked[:, half * head_size : (half + 1) * head_size], preferred_element_type=jnp.float32)
-            if distance > HALF:
-                grad_send[distance, half] = part.astype(jnp.bfloat16)
-            else:
-                grad_window[half, block, :] = part
+            part = jnp.dot(left[span, :], stacked[...], preferred_element_type=jnp.float32)
+            part = part[:, half * head_size : (half + 1) * head_size]
+            for distance in distances:
+                local = (PLACES[distance] - first) * rows
+                piece = part[local : local + rows, :]
+                if distance > HALF:
+                    grad_send[distance, half] = piece.astype(jnp.bfloat16)
+                else:
+                    grad_window[half, block_rows(distance), :] = piece
 
     def send_far(distance):
         @pl.when(me >= distance)
@@ -335,24 +343,24 @@
             out_ref[:, first : first + head_size] = out_part[:, local].T
             grad_queries_ref[:, first : first + head_size] = grad_part[:, local].T
 
-    for distance in (7, 6, 5, 8):
-        grad_block(distance)
-        send_far(distance)
-    grad_block(3)
-    grad_block(2)
-    grad_block(1)
+    grad_blocks(6, 7)
+    send_far(7)
+    send_far(6)
+    grad_blocks(5)
+    send_far(5)
+    grad_blocks(8)
+    send_far(8)
+    grad_blocks(2, 3)
     send_near(3)
-    grad_block(4)
-    grad_block(0)
     send_near(2)
-    pending = list(range(groups))
-    early = groups // 2
-    for group in pending[:early]:
-        finish(group)
+    grad_blocks(1, 4)
     send_near(1)
-    for group in pending[early:]:
-        finish(group)
     send_near(4)
+    grad_blocks(0)
+    finish(0)
+    finish(1)
+    finish(2)
+    finish(3)
 
     for distance in range(1, HALF + 1):
 

time: 27.4 us -> 26.5 us (0.967)
  Pallas kernels: 26.2 us -> 25.4 us
    pallas_call x1, Pallas kernels: 25.2 us -> 24.4 us  [per_device(): pl.pallas_call(functools.partial(kernel, count, members), out_shape=tuple...]
where the time goes in v3:
time: 26.5 us; the launch traced here: 26.1 us
  Pallas kernels  25.4 us (96%)
  between operations  0.64 us (2%)
    pallas_call x1, Pallas kernels, per_device(): pl.pallas_call(functools.partial(kernel, count, members), out_shape=tuple...  24.4 us
    pallas_call x1, Pallas kernels, per_device(): pl.pallas_call(settle, out_shape=tuple((jax.ShapeDtypeStruct(result.shape...  1.01 us

profile of v3, /device:TPU:1, one launch (start us, length us, event | category | flops | bytes accessed | tf_op | source)
XLA Modules:
  0.0 26.1 jit_solution(1250993681222781439)
XLA Ops:
  0.6 24.4 %attention.1 = (bf16[128,2048]{1,0:T(8,128)(2,1)S(1)}, bf16[128,2048]{1,0:T(8,128)(2,1)S(1)}, bf16[128,128]{1,0:T(8,128)(2,1)S(1)}, bf16[128,128]{1,0:T(8,128)(2,1)S(1)}) custom-call(s32[8]{0:T(128)} %lengths_hbm.1, bf16[128,2048]{1,0:T(8,128)(2,1)} %queries_hbm.1, bf16[128,128]{1,0:T(8,128)(2,1)} %keys_hbm.1, bf16[128,128]{1,0:T(8,128)(2,1)} %values_hbm.1, ...), custom_call_target="tpu_custom_call" | custom-call | tf_op jit(solution)/shard_map/attention/pallas_call | solution.py:426
  25.1 1.0 %settle.1 = (bf16[128,2048]{1,0:T(8,128)(2,1)}, bf16[128,2048]{1,0:T(8,128)(2,1)}, bf16[128,128]{1,0:T(8,128)(2,1)}, bf16[128,128]{1,0:T(8,128)(2,1)}) custom-call(bf16[128,2048]{1,0:T(8,128)(2,1)S(1)} %get-tuple-element.8.refs_0_, bf16[128,2048]{1,0:T(8,128)(2,1)S(1)} %get-tuple-element.9.refs_1_, bf16[128,128]{1,0:T(8,128)(2,1)S(1)} %get-tuple-element.10.refs_2_, ...), custom_call_target="tpu_custom_call" | custom-call | tf_op jit(solution)/shard_map/settle/pallas_call | solution.py:466

commit v4 on v3

--- a/solution.py
+++ b/solution.py
@@ -9,7 +9,7 @@
 
 REACH = 8
 HALF = REACH // 2
-GROUP_HEADS = 4
+GROUP_HEADS = 8
 MASKED = -1e30
 LOG2E = 1.4426950408889634
 PLACES = (0, 1, 3, 4, 2, 5, 6, 7, 8)
@@ -343,24 +343,21 @@
             out_ref[:, first : first + head_size] = out_part[:, local].T
             grad_queries_ref[:, first : first + head_size] = grad_part[:, local].T
 
-    grad_blocks(6, 7)
+    grad_blocks(7, 8)
     send_far(7)
+    send_far(8)
+    grad_blocks(5, 6)
     send_far(6)
-    grad_blocks(5)
     send_far(5)
-    grad_blocks(8)
-    send_far(8)
     grad_blocks(2, 3)
     send_near(3)
     send_near(2)
     grad_blocks(1, 4)
     send_near(1)
-    send_near(4)
     grad_blocks(0)
     finish(0)
+    send_near(4)
     finish(1)
-    finish(2)
-    finish(3)
 
     for distance in range(1, HALF + 1):
 

time: 26.5 us -> 26.5 us (level)
  the two profiles are of different devices: /device:TPU:1 before, /device:TPU:27 now
where the time goes in v4:
time: 26.5 us; the launch traced here: 26.3 us
  Pallas kernels  25.6 us (97%)
  between operations  0.64 us (2%)
    pallas_call x1, Pallas kernels, per_device(): pl.pallas_call(functools.partial(kernel, count, members), out_shape=tuple...  24.6 us
    pallas_call x1, Pallas kernels, per_device(): pl.pallas_call(settle, out_shape=tuple((jax.ShapeDtypeStruct(result.shape...  1.01 us

profile of v4, /device:TPU:27, one launch (start us, length us, event | category | flops | bytes accessed | tf_op | source)
XLA Modules:
  0.0 26.3 jit_solution(12129723172293469486)
XLA Ops:
  0.6 24.6 %attention.1 = (bf16[128,2048]{1,0:T(8,128)(2,1)S(1)}, bf16[128,2048]{1,0:T(8,128)(2,1)S(1)}, bf16[128,128]{1,0:T(8,128)(2,1)S(1)}, bf16[128,128]{1,0:T(8,128)(2,1)S(1)}) custom-call(s32[8]{0:T(128)} %lengths_hbm.1, bf16[128,2048]{1,0:T(8,128)(2,1)} %queries_hbm.1, bf16[128,128]{1,0:T(8,128)(2,1)} %keys_hbm.1, bf16[128,128]{1,0:T(8,128)(2,1)} %values_hbm.1, ...), custom_call_target="tpu_custom_call" | custom-call | tf_op jit(solution)/shard_map/attention/pallas_call | solution.py:423
  25.3 1.0 %settle.1 = (bf16[128,2048]{1,0:T(8,128)(2,1)}, bf16[128,2048]{1,0:T(8,128)(2,1)}, bf16[128,128]{1,0:T(8,128)(2,1)}, bf16[128,128]{1,0:T(8,128)(2,1)}) custom-call(bf16[128,2048]{1,0:T(8,128)(2,1)S(1)} %get-tuple-element.8.refs_0_, bf16[128,2048]{1,0:T(8,128)(2,1)S(1)} %get-tuple-element.9.refs_1_, bf16[128,128]{1,0:T(8,128)(2,1)S(1)} %get-tuple-element.10.refs_2_, ...), custom_call_target="tpu_custom_call" | custom-call | tf_op jit(solution)/shard_map/settle/pallas_call | solution.py:463
